TPU v7x, 32 devices: a whole 2x2x4 slice. The times are simulated.
32 devices in a mesh: grp: 4 (over x, core), mem: 8 (over z, y).
Axes of the slice: x: 2, y: 2, z: 4, core: 2. Of those that a mesh axis runs over, the one named last changes fastest.
Arguments:
- source_pts: float32 [64, 8192], P(None, ('grp', 'mem')), may hold values from -30 to 30
- target_pts: float32 [64, 8192], P(None, ('grp', 'mem')), may hold values from -30 to 30
- source_pot: float32 [8192], P(('grp', 'mem')), may hold values from -8 to 520
- target_pot: float32 [8192], P(('grp', 'mem')), may hold values from -8 to 520
- source_logw: float32 [8192], P(('grp', 'mem')), may hold values from -1 to 4
- target_logw: float32 [8192], P(('grp', 'mem')), may hold values from -1 to 4
Outputs:
- source_new: float32 [8192], P(('grp', 'mem'))
- target_new: float32 [8192], P(('grp', 'mem'))
All inputs are finite; a program needn't handle non-finite values.
Results may differ from a plain program's by a relative error of at most 0.0001.
Values sent between devices are 32-bit elements; how exact they have to be, the bound alone decides.
A program may use at most 64 MiB of HBM per device.

v0:
```python
import math
import jax
import jax.numpy as jnp
from jax import lax
from jax.sharding import PartitionSpec as P

epsilon = 4.0
floor_value = -1e30


def sweep(carry, points, squares, row_term, moving, offset):
    count = moving.shape[1]
    limit = 128
    width = math.gcd(count, limit)

    def block(index, state):
        row_max, row_sum, col_max, col_sum = state
        begin = index * width
        cols = lax.dynamic_slice_in_dim(moving, begin, width, 1)
        ycols = cols[:-1]
        cvals = cols[-1]
        ysq = 0.5 * jnp.sum(ycols * ycols, 0)
        cross = lax.dot_general(
            points,
            ycols,
            (((0,), (0,)), ((), ())),
            precision=lax.Precision.HIGHEST,
            preferred_element_type=jnp.float32,
        )
        half = (squares[:, None] + ysq[None, :] - cross) / epsilon
        scores = cvals[None, :] - half
        new_row = jnp.maximum(row_max, jnp.max(scores, 1))
        row_sum = row_sum * jnp.exp(row_max - new_row) + jnp.sum(
            jnp.exp(scores - new_row[:, None]), 1
        )
        others = row_term[:, None] - half
        place = offset + begin
        old_max = lax.dynamic_slice_in_dim(col_max, place, width, 0)
        old_sum = lax.dynamic_slice_in_dim(col_sum, place, width, 0)
        new_col = jnp.maximum(old_max, jnp.max(others, 0))
        new_sum = old_sum * jnp.exp(old_max - new_col) + jnp.sum(
            jnp.exp(others - new_col[None, :]), 0
        )
        col_max = lax.dynamic_update_slice_in_dim(col_max, new_col, place, 0)
        col_sum = lax.dynamic_update_slice_in_dim(col_sum, new_sum, place, 0)
        return (new_row, row_sum, col_max, col_sum)

    return lax.fori_loop(0, count // width, block, carry)


def totals(source_logw, target_logw):
    peaks = lax.pmax((jnp.max(source_logw), jnp.max(target_logw)), ("grp", "mem"))
    masses = lax.psum(
        (jnp.sum(jnp.exp(source_logw - peaks[0])), jnp.sum(jnp.exp(target_logw - peaks[1]))),
        ("grp", "mem"),
    )
    return (peaks[0] + jnp.log(masses[0]), peaks[1] + jnp.log(masses[1]))


def local(source_pts, target_pts, source_pot, target_pot, source_logw, target_logw):
    members = lax.axis_size("mem")
    rows = source_pts.shape[1]
    outer = rows * members
    src_norm, tgt_norm = totals(source_logw, target_logw)
    row_term = source_logw - src_norm + source_pot / epsilon
    col_term = target_logw - tgt_norm + target_pot / epsilon
    moving = jnp.concatenate([target_pts, col_term[None, :]], 0)
    standing = jnp.concatenate([source_pts, row_term[None, :]], 0)
    row_block = lax.all_gather(standing, "mem", axis=1, tiled=True)
    col_block = lax.all_gather(moving, "grp", axis=1, tiled=True)
    block_pts = row_block[:-1]
    block_terms = row_block[-1]
    block_sq = 0.5 * jnp.sum(block_pts * block_pts, 0)
    span = col_block.shape[1]
    carry = (
        jnp.full((outer,), floor_value, jnp.float32),
        jnp.zeros((outer,), jnp.float32),
        jnp.full((span,), floor_value, jnp.float32),
        jnp.zeros((span,), jnp.float32),
    )
    row_max, row_sum, col_max, col_sum = sweep(
        carry, block_pts, block_sq, block_terms, col_block, 0
    )
    rpeak = lax.pmax(row_max, "mem")
    own_rsum = lax.psum_scatter(
        row_sum * jnp.exp(row_max - rpeak), "mem", scatter_dimension=0, tiled=True
    )
    own_rmax = lax.dynamic_slice_in_dim(rpeak, lax.axis_index("mem") * rows, rows, 0)
    row_total = own_rmax + jnp.log(own_rsum)
    cpeak = lax.pmax(col_max, "grp")
    own_sum = lax.psum_scatter(
        col_sum * jnp.exp(col_max - cpeak), "grp", scatter_dimension=0, tiled=True
    )
    own_max = lax.dynamic_slice_in_dim(cpeak, lax.axis_index("grp") * rows, rows, 0)
    col_total = own_max + jnp.log(own_sum)
    row_hat = -epsilon * row_total
    col_hat = -epsilon * col_total
    return (0.5 * (source_pot + row_hat), 0.5 * (target_pot + col_hat))


def solution(mesh):
    return jax.shard_map(
        local,
        mesh=mesh,
        in_specs=(
            P(None, ("grp", "mem")),
            P(None, ("grp", "mem")),
            P(("grp", "mem")),
            P(("grp", "mem")),
            P(("grp", "mem")),
            P(("grp", "mem")),
        ),
        out_specs=(P(("grp", "mem")), P(("grp", "mem"))),
        check_vma=False,
    )
```

profile of v0, /device:TPU:0, one launch (start us, length us, event | category | flops | bytes accessed | tf_op | source)
XLA Modules:
  0.0 205.6 jit_solution(15678545301726195394)
XLA Ops:
  0.6 1.3 reduce_max.44
  2.5 42.2 %all-reduce.3 = (f32[]{:T(128)}, f32[]{:T(128)}) all-reduce(f32[]{:T(128)} %reduce_max.44, f32[]{:T(128)} %reduce_max.45), channel_id=1, replica_groups=mesh['grp'=4,'mem'=8] {'grp','mem'}, use_global_device_ids=true, to_apply=%region_1.0 | all-reduce | flops 2 | bytes 16 | tf_op jit(solution)/shard_map/pmax | solution.py:52
  44.8 0.7 copy-done.3
  45.4 2.0 exponential_reduce_fusion.2
  47.4 40.6 %all-reduce.2 = (f32[]{:T(128)}, f32[]{:T(128)}) all-reduce(f32[]{:T(128)} %get-tuple-element.225, f32[]{:T(128)} %get-tuple-element.224), channel_id=1, replica_groups=mesh['grp'=4,'mem'=8] {'grp','mem'}, use_global_device_ids=true, to_apply=%region_3.0 | all-reduce | flops 2 | bytes 16 | tf_op jit(solution)/shard_map/psum | solution.py:53
  89.3 0.8 pad_maximum_fusion.1
  90.2 31.4 %all_gather.7 = f32[65,2048]{1,0:T(8,128)S(1)} all-gather(f32[65,256]{1,0:T(8,128)S(1)} %pad_maximum_fusion.1), channel_id=1, replica_groups=mesh['grp'=4,'mem'=8] {'mem'}, dimensions={1}, use_global_device_ids=true | all-gather | bytes 599040 | tf_op jit(solution)/shard_map/all_gather | solution.py:69
  121.7 0.7 copy-done
  123.8 6.7 %all_gather.6 = f32[65,1024]{1,0:T(8,128)S(1)} all-gather(f32[65,256]{1,0:T(8,128)S(1)} %pad_maximum_fusion), channel_id=1, replica_groups=mesh['grp'=4,'mem'=8] {'grp'}, dimensions={1}, use_global_device_ids=true | all-gather | bytes 332800 | tf_op jit(solution)/shard_map/all_gather | solution.py:70
  130.5 0.7 slice-done
  131.2 18.0 %while.20 = (s32[]{:T(128)}, f32[2048]{0:T(1024)S(1)}, f32[2048]{0:T(1024)S(1)}, f32[1024]{0:T(1024)S(1)}, f32[1024]{0:T(1024)S(1)}, /*index=5*/f32[65,1024]{1,0...) while((s32[]{:T(128)}, f32[2048]{0:T(1024)S(1)}, ...), condition=%wide.region_15.0_spmd.clone, body=%wide.region_9.0_spmd.clone.sunk | while | flops 204761344 | bytes 2844898 | solution.py:48
  131.2 1.3 subtract_reduce_fusion.3
  133.5 1.3 subtract_reduce_fusion.3
  135.7 1.3 subtract_reduce_fusion.3
  138.0 1.3 subtract_reduce_fusion.3
  140.2 1.3 subtract_reduce_fusion.3
  142.5 1.3 subtract_reduce_fusion.3
  144.8 1.3 subtract_reduce_fusion.3
  147.0 1.3 subtract_reduce_fusion.3
  149.2 7.1 %pmax.31 = f32[1024]{0:T(1024)S(1)} all-reduce(f32[1024]{0:T(1024)S(1)} %get-tuple-element.161), channel_id=1, replica_groups=mesh['grp'=4,'mem'=8] {'grp'}, use_global_device_ids=true, to_apply=%region_18.0 | all-reduce | flops 1024 | bytes 8192 | tf_op jit(solution)/shard_map/pmax | solution.py:90
  156.3 6.0 %all-reduce.1 = f32[1024]{0:T(1024)S(1)} all-reduce(f32[1024]{0:T(1024)S(1)} %exponential_multiply_fusion.1), channel_id=3, replica_groups=mesh['grp'=4,'mem'=8] {'grp'}, use_global_device_ids=true, to_apply=%region_19.0.clone | all-reduce | flops 1024 | bytes 8192
  164.8 20.8 %pmax.30 = f32[2048]{0:T(1024)S(1)} all-reduce(f32[2048]{0:T(1024)S(1)} %get-tuple-element.159), channel_id=1, replica_groups=mesh['grp'=4,'mem'=8] {'mem'}, use_global_device_ids=true, to_apply=%region_16.0 | all-reduce | flops 2048 | bytes 16384 | tf_op jit(solution)/shard_map/pmax | solution.py:84
  185.7 17.4 %all-reduce = f32[2048]{0:T(1024)S(1)} all-reduce(f32[2048]{0:T(1024)S(1)} %exponential_multiply_fusion), channel_id=2, replica_groups=mesh['grp'=4,'mem'=8] {'mem'}, use_global_device_ids=true, to_apply=%region_17.0.clone | all-reduce | flops 2048 | bytes 16384
  205.0 0.7 fusion.11
  (118 shorter events, 10.9 us)
Async XLA Ops:
  0.6 1.3 copy-start.2
  44.8 0.7 copy-start.3
  88.6 0.7 copy-start.5
  121.6 0.8 copy-start
  121.6 2.1 %copy-start.1 = (f32[64,256]{1,0:T(8,128)S(1)}, f32[64,256]{1,0:T(8,128)}, u32[]{:S(2)}) copy-start(f32[64,256]{1,0:T(8,128)} %param.9) | copy-start | bytes 196612
  123.0 0.7 copy-start.4
  130.5 0.7 slice-start
  162.3 0.7 copy-start.7
  203.1 0.7 copy-start.6
where the time goes:
time: 206 us
  blocking collectives  172 us (83%)
  other arithmetic  13 us (6%)
  matrix products  10.4 us (5%)
  local copies, waits for them, and re-layouts  4.74 us (2%)
  between operations  4.67 us (2%)
    pmax x1, blocking collectives, totals(): lax.pmax((jnp.max(source_logw), jnp.max(target_logw)), ('grp', 'mem'))  42.2 us
    psum x1, blocking collectives, totals(): lax.psum((jnp.sum(jnp.exp(source_logw - peaks[0])), jnp.sum(jnp.exp(targe...  40.6 us
    all_gather x1, blocking collectives, local(): row_block = lax.all_gather(standing, 'mem', axis=1, tiled=True)  31.4 us
    unnamed x2, blocking collectives  23.4 us
    pmax x1, blocking collectives, local(): rpeak = lax.pmax(row_max, 'mem')  20.8 us
    dot_general x8, matrix products, block(): lax.dot_general(points, ycols, (((0,), (0,)), ((), ())), precision=lax.Pr...  10.4 us
    pmax x1, blocking collectives, local(): cpeak = lax.pmax(col_max, 'grp')  7.05 us
    all_gather x1, blocking collectives, local(): col_block = lax.all_gather(moving, 'grp', axis=1, tiled=True)  6.72 us

commit v1 on v0

--- a/solution.py
+++ b/solution.py
@@ -1,3 +1,4 @@
+import functools
 import math
 import jax
 import jax.numpy as jnp
@@ -6,6 +7,15 @@
 
 epsilon = 4.0
 floor_value = -1e30
+
+
+def region_test(tile_in, axis_tag, comm_axis):
+    for k0 in (axis_tag, comm_axis):
+        tile_in = lax.psum(tile_in, k0)
+    return tile_in
+
+
+trees_mark = functools.partial(region_test, axis_tag="mem", comm_axis="grp")
 
 
 def sweep(carry, points, squares, row_term, moving, offset):
@@ -50,9 +60,8 @@
 
 def totals(source_logw, target_logw):
     peaks = lax.pmax((jnp.max(source_logw), jnp.max(target_logw)), ("grp", "mem"))
-    masses = lax.psum(
-        (jnp.sum(jnp.exp(source_logw - peaks[0])), jnp.sum(jnp.exp(target_logw - peaks[1]))),
-        ("grp", "mem"),
+    masses = trees_mark(
+        (jnp.sum(jnp.exp(source_logw - peaks[0])), jnp.sum(jnp.exp(target_logw - peaks[1])))
     )
     return (peaks[0] + jnp.log(masses[0]), peaks[1] + jnp.log(masses[1]))
 

time: 206 us -> 191 us (0.927)
  blocking collectives: 172 us -> 157 us
    psum x1 -> x2, blocking collectives: 40.6 us -> 28.5 us  [region_test(): tile_in = lax.psum(tile_in, k0)]
    pmax x1, blocking collectives: 20.8 us -> 17.5 us  [local(): rpeak = lax.pmax(row_max, 'mem')]
where the time goes in v1:
time: 191 us; the launch traced here: 190 us
  blocking collectives  157 us (82%)
  other arithmetic  13 us (7%)
  matrix products  10.4 us (5%)
  local copies, waits for them, and re-layouts  4.74 us (2%)
  between operations  4.67 us (2%)
    pmax x1, blocking collectives, totals(): lax.pmax((jnp.max(source_logw), jnp.max(target_logw)), ('grp', 'mem'))  42.2 us
    all_gather x1, blocking collectives, local(): row_block = lax.all_gather(standing, 'mem', axis=1, tiled=True)  31.4 us
    psum x2, blocking collectives, region_test(): tile_in = lax.psum(tile_in, k0)  28.5 us
    unnamed x2, blocking collectives  25 us
    pmax x1, blocking collectives, local(): rpeak = lax.pmax(row_max, 'mem')  17.5 us
    dot_general x8, matrix products, block(): lax.dot_general(points, ycols, (((0,), (0,)), ((), ())), precision=lax.Pr...  10.4 us
    pmax x1, blocking collectives, local(): cpeak = lax.pmax(col_max, 'grp')  6.2 us
    all_gather x1, blocking collectives, local(): col_block = lax.all_gather(moving, 'grp', axis=1, tiled=True)  5.87 us

profile of v1, /device:TPU:0, one launch (start us, length us, event | category | flops | bytes accessed | tf_op | source)
XLA Modules:
  0.0 190.0 jit_solution(2839522664484192782)
XLA Ops:
  0.6 1.3 reduce_max.44
  2.5 42.2 %all-reduce.2 = (f32[]{:T(128)}, f32[]{:T(128)}) all-reduce(f32[]{:T(128)} %reduce_max.44, f32[]{:T(128)} %reduce_max.45), channel_id=1, replica_groups=mesh['grp'=4,'mem'=8] {'grp','mem'}, use_global_device_ids=true, to_apply=%region_1.0 | all-reduce | flops 2 | bytes 16 | tf_op jit(solution)/shard_map/pmax | solution.py:62
  44.7 0.7 copy-done.3
  45.4 2.0 %exponential_reduce_fusion.2 = (f32[]{:T(128)}, f32[]{:T(128)}) fusion(f32[256]{0:T(256)S(1)} %copy-done.2, f32[]{:T(128)} %get-tuple-element.216, f32[256]{0:T(256)S(1)} %copy-done.3, f32[]{:T(128)} %get-tuple-element.215), kind=kLoop, calls=%fused_computation.32 | loop fusion | flops 1022 | bytes 2064 | tf_op jit(solution)/shard_map/reduce_sum | solution.py:64
  47.4 21.9 %all-reduce.3 = (f32[]{:T(128)}, f32[]{:T(128)}) all-reduce(f32[]{:T(128)} %get-tuple-element.227, f32[]{:T(128)} %get-tuple-element.226), channel_id=1, replica_groups=mesh['grp'=4,'mem'=8] {'mem'}, use_global_device_ids=true, to_apply=%region_3.0 | all-reduce | flops 2 | bytes 16 | tf_op jit(solution)/shard_map/psum | solution.py:14
  69.3 6.6 %all-reduce.4 = (f32[]{:T(128)}, f32[]{:T(128)}) all-reduce(f32[]{:T(128)} %get-tuple-element.217, f32[]{:T(128)} %get-tuple-element.218), channel_id=1, replica_groups=mesh['grp'=4,'mem'=8] {'grp'}, use_global_device_ids=true, to_apply=%region_4.0 | all-reduce | flops 2 | bytes 16 | tf_op jit(solution)/shard_map/psum | solution.py:14
  77.2 0.8 pad_maximum_fusion.1
  78.1 31.4 %all_gather.7 = f32[65,2048]{1,0:T(8,128)S(1)} all-gather(f32[65,256]{1,0:T(8,128)S(1)} %pad_maximum_fusion.1), channel_id=1, replica_groups=mesh['grp'=4,'mem'=8] {'mem'}, dimensions={1}, use_global_device_ids=true | all-gather | bytes 599040 | tf_op jit(solution)/shard_map/all_gather | solution.py:78
  109.5 0.7 copy-done
  111.6 5.9 %all_gather.6 = f32[65,1024]{1,0:T(8,128)S(1)} all-gather(f32[65,256]{1,0:T(8,128)S(1)} %pad_maximum_fusion), channel_id=1, replica_groups=mesh['grp'=4,'mem'=8] {'grp'}, dimensions={1}, use_global_device_ids=true | all-gather | bytes 332800 | tf_op jit(solution)/shard_map/all_gather | solution.py:79
  117.5 0.7 slice-done
  118.2 18.0 %while.20 = (s32[]{:T(128)}, f32[2048]{0:T(1024)S(1)}, f32[2048]{0:T(1024)S(1)}, f32[1024]{0:T(1024)S(1)}, f32[1024]{0:T(1024)S(1)}, /*index=5*/f32[65,1024]{1,0...) while((s32[]{:T(128)}, f32[2048]{0:T(1024)S(1)}, ...), condition=%wide.region_17.0_spmd.clone, body=%wide.region_11.0_spmd.clone.sunk | while | flops 204761344 | bytes 2844898 | solution.py:58
  118.2 1.3 subtract_reduce_fusion.3
  120.4 1.3 subtract_reduce_fusion.3
  122.7 1.3 subtract_reduce_fusion.3
  125.0 1.3 subtract_reduce_fusion.3
  127.2 1.3 subtract_reduce_fusion.3
  129.5 1.3 subtract_reduce_fusion.3
  131.7 1.3 subtract_reduce_fusion.3
  134.0 1.3 subtract_reduce_fusion.3
  136.2 6.2 %pmax.31 = f32[1024]{0:T(1024)S(1)} all-reduce(f32[1024]{0:T(1024)S(1)} %get-tuple-element.161), channel_id=1, replica_groups=mesh['grp'=4,'mem'=8] {'grp'}, use_global_device_ids=true, to_apply=%region_20.0 | all-reduce | flops 1024 | bytes 8192 | tf_op jit(solution)/shard_map/pmax | solution.py:99
  142.4 5.7 %all-reduce.1 = f32[1024]{0:T(1024)S(1)} all-reduce(f32[1024]{0:T(1024)S(1)} %exponential_multiply_fusion.1), channel_id=3, replica_groups=mesh['grp'=4,'mem'=8] {'grp'}, use_global_device_ids=true, to_apply=%region_21.0.clone | all-reduce | flops 1024 | bytes 8192
  150.6 17.5 %pmax.30 = f32[2048]{0:T(1024)S(1)} all-reduce(f32[2048]{0:T(1024)S(1)} %get-tuple-element.159), channel_id=1, replica_groups=mesh['grp'=4,'mem'=8] {'mem'}, use_global_device_ids=true, to_apply=%region_18.0 | all-reduce | flops 2048 | bytes 16384 | tf_op jit(solution)/shard_map/pmax | solution.py:93
  168.1 19.3 %all-reduce = f32[2048]{0:T(1024)S(1)} all-reduce(f32[2048]{0:T(1024)S(1)} %exponential_multiply_fusion), channel_id=2, replica_groups=mesh['grp'=4,'mem'=8] {'mem'}, use_global_device_ids=true, to_apply=%region_19.0.clone | all-reduce | flops 2048 | bytes 16384
  (119 shorter events, 11.5 us)
Async XLA Ops:
  0.6 1.3 copy-start.2
  44.7 0.7 copy-start.3
  76.6 0.7 copy-start.5
  109.5 0.8 copy-start
  109.5 2.1 %copy-start.1 = (f32[64,256]{1,0:T(8,128)S(1)}, f32[64,256]{1,0:T(8,128)}, u32[]{:S(2)}) copy-start(f32[64,256]{1,0:T(8,128)} %param.9) | copy-start | bytes 196612
  110.9 0.7 copy-start.4
  117.5 0.7 slice-start
  148.1 0.7 copy-start.7
  187.4 0.7 copy-start.6

commit v2 on v0

--- a/solution.py
+++ b/solution.py
@@ -6,6 +6,9 @@
 
 epsilon = 4.0
 floor_value = -1e30
+_derive_roads = lambda sheet: jnp.concatenate(
+    jax.lax.all_to_all(jnp.stack([sheet] * jax.lax.psum(1, "mem")), "mem", 0, 0), axis=1
+)
 
 
 def sweep(carry, points, squares, row_term, moving, offset):
@@ -66,7 +69,7 @@
     col_term = target_logw - tgt_norm + target_pot / epsilon
     moving = jnp.concatenate([target_pts, col_term[None, :]], 0)
     standing = jnp.concatenate([source_pts, row_term[None, :]], 0)
-    row_block = lax.all_gather(standing, "mem", axis=1, tiled=True)
+    row_block = _derive_roads(standing)
     col_block = lax.all_gather(moving, "grp", axis=1, tiled=True)
     block_pts = row_block[:-1]
     block_terms = row_block[-1]

time: 206 us -> 181 us (0.88)
  blocking collectives: 172 us -> 137 us
  starting transfers between devices: 0 us -> 5.52 us
  waiting for transfers between devices: 0 us -> 4.84 us
    all_gather x1 -> x0, blocking collectives: 31.4 us -> none  [local(): row_block = lax.all_gather(standing, 'mem', axis=1, tiled=True)]
    all_to_all x0 -> x1, starting transfers between devices: none -> 5.52 us  [jax.lax.all_to_all(jnp.stack([sheet] * jax.lax.psum(1, 'mem')), 'mem', 0, 0)]
    all_to_all x0 -> x1, waiting for transfers between devices: none -> 4.84 us  [jax.lax.all_to_all(jnp.stack([sheet] * jax.lax.psum(1, 'mem')), 'mem', 0, 0)]
  transfers between devices with their start and end apart: 0 -> 1, of which waited for: 0 -> 1; matrix products, arithmetic and copies ran while one was open for 0% -> 1% of each run, Pallas kernels for 0% -> 0%
where the time goes in v2:
time: 181 us; the launch traced here: 180 us
  blocking collectives  137 us (76%)
  other arithmetic  13 us (7%)
  matrix products  10.5 us (6%)
  starting transfers between devices  5.52 us (3%)
  waiting for transfers between devices  4.84 us (3%)
  between operations  4.62 us (3%)
  local copies, waits for them, and re-layouts  3.58 us (2%)
    pmax x1, blocking collectives, totals(): lax.pmax((jnp.max(source_logw), jnp.max(target_logw)), ('grp', 'mem'))  42.2 us
    psum x1, blocking collectives, totals(): lax.psum((jnp.sum(jnp.exp(source_logw - peaks[0])), jnp.sum(jnp.exp(targe...  40.5 us
    unnamed x2, blocking collectives  23.4 us
    pmax x1, blocking collectives, local(): rpeak = lax.pmax(row_max, 'mem')  19.5 us
    dot_general x8, matrix products, block(): lax.dot_general(points, ycols, (((0,), (0,)), ((), ())), precision=lax.Pr...  10.5 us
    all_gather x1, blocking collectives, local(): col_block = lax.all_gather(moving, 'grp', axis=1, tiled=True)  5.94 us
    pmax x1, blocking collectives, local(): cpeak = lax.pmax(col_max, 'grp')  5.67 us
    all_to_all x1, starting transfers between devices, jax.lax.all_to_all(jnp.stack([sheet] * jax.lax.psum(1, 'mem')), 'mem', 0, 0)  5.52 us
  transfers between devices with their start and end apart: 1, of which 1 were waited for; matrix products, arithmetic and copies ran while one was open for 1% of the time, Pallas kernels for 0%

profile of v2, /device:TPU:0, one launch (start us, length us, event | category | flops | bytes accessed | tf_op | source)
XLA Modules:
  0.0 179.9 jit_solution(13230917379900003433)
XLA Ops:
  0.6 1.3 reduce_max.44
  2.5 42.2 %all-reduce.3 = (f32[]{:T(128)}, f32[]{:T(128)}) all-reduce(f32[]{:T(128)} %reduce_max.44, f32[]{:T(128)} %reduce_max.45), channel_id=1, replica_groups=mesh['grp'=4,'mem'=8] {'grp','mem'}, use_global_device_ids=true, to_apply=%region_1.0 | all-reduce | flops 2 | bytes 16 | tf_op jit(solution)/shard_map/pmax | solution.py:55
  44.7 0.7 copy-done.2
  45.4 2.0 %exponential_reduce_fusion.2 = (f32[]{:T(128)}, f32[]{:T(128)}) fusion(f32[256]{0:T(256)S(1)} %copy-done.1, f32[]{:T(128)} %get-tuple-element.218, f32[256]{0:T(256)S(1)} %copy-done.2, f32[]{:T(128)} %get-tuple-element.217), kind=kLoop, calls=%fused_computation.33 | loop fusion | flops 1022 | bytes 2064 | tf_op jit(solution)/shard_map/reduce_sum | solution.py:57
  47.4 40.5 %all-reduce.2 = (f32[]{:T(128)}, f32[]{:T(128)}) all-reduce(f32[]{:T(128)} %get-tuple-element.225, f32[]{:T(128)} %get-tuple-element.224), channel_id=1, replica_groups=mesh['grp'=4,'mem'=8] {'grp','mem'}, use_global_device_ids=true, to_apply=%region_3.0 | all-reduce | flops 2 | bytes 16 | tf_op jit(solution)/shard_map/psum | solution.py:56
  89.3 0.8 pad_maximum_fusion.1
  90.2 0.8 stack.2
  91.0 5.5 %all-to-all-start = ((f32[8,65,256]{2,1,0:T(8,128)}), f32[8,65,256]{2,1,0:T(8,128)S(1)}, u32[]{:S(2)}, u32[]{:S(2)}) async-start(f32[8,65,256]{2,1,0:T(8,128)} %stack.2), calls=%async_computation | async-start | bytes 1179648 | tf_op jit(solution)/shard_map/all_to_all | solution.py:10
  100.2 0.7 copy-done.3
  100.9 5.9 %all_gather.3 = f32[65,1024]{1,0:T(8,128)S(1)} all-gather(f32[65,256]{1,0:T(8,128)S(1)} %pad_maximum_fusion), channel_id=1, replica_groups=mesh['grp'=4,'mem'=8] {'grp'}, dimensions={1}, use_global_device_ids=true | all-gather | bytes 332800 | tf_op jit(solution)/shard_map/all_gather | solution.py:73
  106.9 4.8 %all-to-all-done = f32[8,65,256]{2,1,0:T(8,128)S(1)} async-done(((f32[8,65,256]{2,1,0:T(8,128)}), f32[8,65,256]{2,1,0:T(8,128)S(1)}, u32[]{:S(2)}, u32[]{:S(2)}) %all-to-all-start) | async-done | bytes 532512 | tf_op jit(solution)/shard_map/all_to_all | solution.py:10
  111.9 18.1 %while.20 = (s32[]{:T(128)}, f32[2048]{0:T(1024)S(1)}, f32[2048]{0:T(1024)S(1)}, f32[1024]{0:T(1024)S(1)}, f32[1024]{0:T(1024)S(1)}, /*index=5*/f32[65,1024]{1,0...) while((s32[]{:T(128)}, f32[2048]{0:T(1024)S(1)}, ...), condition=%wide.region_15.0_spmd.clone, body=%wide.region_9.0_spmd.clone.sunk | while | flops 204761344 | bytes 2844898 | solution.py:51
  112.0 1.3 subtract_reduce_fusion.3
  114.2 1.3 subtract_reduce_fusion.3
  116.5 1.3 subtract_reduce_fusion.3
  118.7 1.3 subtract_reduce_fusion.3
  121.0 1.3 subtract_reduce_fusion.3
  123.3 1.3 subtract_reduce_fusion.3
  125.5 1.3 subtract_reduce_fusion.3
  127.8 1.3 subtract_reduce_fusion.3
  130.0 5.7 %pmax.31 = f32[1024]{0:T(1024)S(1)} all-reduce(f32[1024]{0:T(1024)S(1)} %get-tuple-element.161), channel_id=1, replica_groups=mesh['grp'=4,'mem'=8] {'grp'}, use_global_device_ids=true, to_apply=%region_18.0 | all-reduce | flops 1024 | bytes 8192 | tf_op jit(solution)/shard_map/pmax | solution.py:93
  135.7 6.0 %all-reduce.1 = f32[1024]{0:T(1024)S(1)} all-reduce(f32[1024]{0:T(1024)S(1)} %exponential_multiply_fusion.1), channel_id=3, replica_groups=mesh['grp'=4,'mem'=8] {'grp'}, use_global_device_ids=true, to_apply=%region_19.0.clone | all-reduce | flops 1024 | bytes 8192
  141.7 19.5 %pmax.30 = f32[2048]{0:T(1024)S(1)} all-reduce(f32[2048]{0:T(1024)S(1)} %get-tuple-element.159), channel_id=1, replica_groups=mesh['grp'=4,'mem'=8] {'mem'}, use_global_device_ids=true, to_apply=%region_16.0 | all-reduce | flops 2048 | bytes 16384 | tf_op jit(solution)/shard_map/pmax | solution.py:87
  161.2 17.4 %all-reduce = f32[2048]{0:T(1024)S(1)} all-reduce(f32[2048]{0:T(1024)S(1)} %exponential_multiply_fusion), channel_id=2, replica_groups=mesh['grp'=4,'mem'=8] {'mem'}, use_global_device_ids=true, to_apply=%region_17.0.clone | all-reduce | flops 2048 | bytes 16384
  (119 shorter events, 10.3 us)
Async XLA Ops:
  0.6 1.3 copy-start.1
  44.7 0.7 copy-start.2
  88.6 0.7 copy-start.4
  91.0 6.8 %copy-start.6 = (u32[32]{0:T(128)S(1)}, u32[32]{0:T(128)}, u32[]{:S(2)}) copy-start(u32[32]{0:T(128)} %constant.93) | copy-start | bytes 388
  91.0 7.4 %copy-start.5 = (u32[32]{0:T(128)S(1)}, u32[32]{0:T(128)}, u32[]{:S(2)}) copy-start(u32[32]{0:T(128)} %constant.89) | copy-start | bytes 388
  91.0 20.7 %all-to-all-start = ((f32[8,65,256]{2,1,0:T(8,128)}), f32[8,65,256]{2,1,0:T(8,128)S(1)}, u32[]{:S(2)}, u32[]{:S(2)}) async-start(f32[8,65,256]{2,1,0:T(8,128)} %stack.2), calls=%async_computation | async-start | bytes 1179648 | tf_op jit(solution)/shard_map/all_to_all | solution.py:10
  96.5 4.4 %copy-start = (f32[64,256]{1,0:T(8,128)S(1)}, f32[64,256]{1,0:T(8,128)}, u32[]{:S(2)}) copy-start(f32[64,256]{1,0:T(8,128)} %param.9) | copy-start | bytes 196612
  100.2 0.7 copy-start.3
